TPU v7x, 32 devices: a whole 2x2x4 slice. The times are simulated.
32 devices in a mesh: dp: 8 (over z, x), mp: 4 (over y, core).
Axes of the slice: x: 2, y: 2, z: 4, core: 2. Of those that a mesh axis runs over, the one named last changes fastest.
Arguments:
- hidden: bfloat16 [2304, 5376], P('dp', 'mp'), may hold values from -6 to 6
- master: float32 [5376, 4096], P(('mp', 'dp')), may hold values from -0.078125 to 0.078125
- grad: float32 [5376, 4096], P(('mp', 'dp')), may hold values from -1500 to 1500, as said below
- row_factor: float32 [5376], P(('mp', 'dp')), may hold values from 0.01 to 1, as said below
- col_factor: float32 [4096], replicated, may hold values from 0.05 to 0.5
Outputs:
- ffn_out: bfloat16 [2304, 4096], P('dp', 'mp')
- update: float32 [5376, 4096], P(('mp', 'dp'))
- row_new: float32 [5376], P(('mp', 'dp'))
- col_new: float32 [4096], replicated
Inputs may be any that keep to these rules, and one draw needn't show every extreme that they name: `grad`: every entry is finite. `row_factor`: every entry is positive.
All inputs are finite; a program needn't handle non-finite values.
Results may differ from a plain program's by a relative error of at most 0.0049.
Values may be sent and summed in bfloat16 or wider, within the bound.
A program may use at most 64 MiB of HBM per device.

v0:
```python
import jax
import jax.numpy as jnp
from jax import lax
from jax.sharding import PartitionSpec as P

D = 4096
FFW = 5376
STEP = 10


def body(hidden, master, grad, row_factor, col_factor):
    keep = 1.0 - STEP ** (-0.8)
    step_rate = min(0.01, STEP ** (-0.5))
    squared = grad * grad + 1e-30
    row_new = keep * row_factor + (1.0 - keep) * jnp.mean(squared, axis=1)
    column_part = jnp.sum(squared, axis=0)
    weighted_part = jnp.sum(grad * grad / row_new[:, None], axis=0)
    column_total, weighted_total = lax.psum((column_part, weighted_part), ("dp", "mp"))
    col_new = keep * col_factor + (1.0 - keep) * column_total / float(FFW)
    scaled = grad * lax.rsqrt(row_new[:, None] * col_new[None, :])
    square_total = jnp.sum(weighted_total / col_new)
    root_mean = jnp.sqrt(square_total / float(FFW * D))
    update = scaled / jnp.maximum(1.0, root_mean)
    weight = (master - step_rate * update).astype(jnp.bfloat16)
    partial_out = jnp.dot(
        hidden, lax.all_gather(weight, "dp", axis=0, tiled=True), preferred_element_type=jnp.float32
    )
    ffn_out = lax.psum_scatter(partial_out, "mp", scatter_dimension=1, tiled=True).astype(
        jnp.bfloat16
    )
    return (ffn_out, update, row_new, col_new)


def solution(mesh):
    return jax.shard_map(
        body,
        mesh=mesh,
        in_specs=(
            P("dp", "mp"),
            P(("mp", "dp"), None),
            P(("mp", "dp"), None),
            P(("mp", "dp")),
            P(),
        ),
        out_specs=(P("dp", "mp"), P(("mp", "dp"), None), P(("mp", "dp")), P()),
        check_vma=False,
    )
```

profile of v0, /device:TPU:0, one launch (start us, length us, event | category | flops | bytes accessed | tf_op | source)
XLA Modules:
  0.0 281.1 jit_solution(14005128101560191098)
XLA Ops:
  7.2 0.0 copy-start
  7.2 0.0 copy-start.5
  7.2 0.0 all-gather.2.cloned.1.call-start
  7.2 0.0 copy-start.1
  7.2 0.0 copy-start.3
  7.3 2.3 add_reduce_fusion.1
  9.5 0.0 copy-done.5
  9.6 0.3 copy-done.1
  9.9 0.0 copy-start.4
  9.9 0.5 add_reduce_fusion
  10.4 42.2 %all-reduce = (f32[4096]{0:T(1024)S(1)}, f32[4096]{0:T(1024)S(1)}) all-reduce(f32[4096]{0:T(1024)S(1)} %get-tuple-element.5, f32[4096]{0:T(1024)S(1)} %get-tuple-element.4), channel_id=1, replica_groups=mesh['dp'=8,'mp'=4] {'dp','mp'}, use_global_device_ids=true, to_apply=%region_4.0 | all-reduce | flops 8192 | bytes 65536 | tf_op jit(solution)/shard_map/psum | solution.py:18
  52.6 0.0 copy-done.3
  52.6 0.6 divide_reduce_fusion.1
  53.3 0.0 copy-start.2
  54.0 5.4 %subtract_convert_fusion = (bf16[168,4096]{1,0:T(8,128)(2,1)}, f32[168,4096]{1,0:T(8,128)}) fusion(f32[168,4096]{1,0:T(8,128)} %param.6, f32[]{:T(128)S(6)} %max_shard_map.3, f32[168,4096]{1,0:T(8,128)} %param.7, f32[4096]{0:T(1024)S(1)} %get-tuple-element.11, f32[168]{0:T(256)S(1)} %multiply_add_fusion.1), kind=kLoop, calls=%fused_computation.1 | loop fusion | flops 4128768 | bytes 9650852 | tf_op jit(solution)/shard_map/convert_element_type | solution.py:24
  59.4 0.0 copy-done.4
  59.4 0.0 copy-done.2
  59.4 0.0 all-gather.2.cloned.1.call-update
  59.4 0.0 reduce-scatter.2.cloned.1.call-start
  59.4 156.8 %all-gather.2.cloned.1.call-done = bf16[1344,4096]{1,0:T(8,128)(2,1)} async-done(((bf16[168,4096]{1,0:T(8,128)(2,1)}), bf16[1344,4096]{1,0:T(8,128)(2,1)}) %all-gather.2.cloned.1.call-update) | async-done | bytes 11010064 | tf_op jit(solution)/shard_map/all_gather | solution.py:26
  216.3 0.0 copy-done
  216.3 9.7 %convolution_bitcast_fusion = f32[288,4096]{1,0:T(8,128)} fusion(bf16[288,1344]{1,0:T(8,128)(2,1)S(1)} %copy-done, bf16[1344,4096]{1,0:T(8,128)(2,1)} %all-gather.2.cloned.1.call-done), kind=kOutput, calls=%fused_computation | convolution fusion | flops 3170893824 | bytes 16502784 | tf_op jit(solution)/shard_map/dot_general | solution.py:25
  225.9 0.0 reduce-scatter.2.cloned.1.call-update
  226.0 46.1 %reduce-scatter.2.cloned.1.call-done = f32[288,1024]{1,0:T(8,128)} async-done(((f32[288,4096]{1,0:T(8,128)}), f32[288,1024]{1,0:T(8,128)}) %reduce-scatter.2.cloned.1.call-update) | async-done | bytes 1179664 | tf_op jit(solution)/shard_map/reduce_scatter | solution.py:28
  272.1 2.2 convert_element_type.7
  (1 shorter events, 0.0 us)
Async XLA Ops:
  7.2 209.1 %copy-start = (bf16[288,1344]{1,0:T(8,128)(2,1)S(1)}, bf16[288,1344]{1,0:T(8,128)(2,1)}, u32[]{:S(2)}) copy-start(bf16[288,1344]{1,0:T(8,128)(2,1)} %param.5) | copy-start | bytes 2322436
  7.2 2.4 copy-start.5
  7.2 209.1 %all-gather.2.cloned.1.call-start = ((), (), s32[]{:S(2)}) async-start(), calls=%async_computation.1 | async-start | bytes 12386304 | tf_op jit(solution)/shard_map/all_gather | solution.py:26
  7.2 2.6 copy-start.1
  7.2 45.4 %copy-start.3 = (f32[4096]{0:T(1024)S(1)}, f32[4096]{0:T(1024)}, u32[]{:S(2)}) copy-start(f32[4096]{0:T(1024)} %param.9) | copy-start | bytes 49156
  9.9 49.5 %copy-start.4 = (f32[168]{0:T(256)}, f32[168]{0:T(256)S(1)}, u32[]{:S(2)}) copy-start(f32[168]{0:T(256)S(1)} %multiply_add_fusion.1) | copy-start | bytes 2020
  53.3 6.1 %copy-start.2 = (f32[4096]{0:T(1024)}, f32[4096]{0:T(1024)S(1)}, u32[]{:S(2)}) copy-start(f32[4096]{0:T(1024)S(1)} %get-tuple-element.11) | copy-start | bytes 49156
  59.4 212.7 %reduce-scatter.2.cloned.1.call-start = ((), (), s32[]{:S(2)}) async-start(), calls=%async_computation.2 | async-start | bytes 5898240 | tf_op jit(solution)/shard_map/reduce_scatter | solution.py:28
Sparse Core Ops, SparseCore 0:
  59.5 156.7 all-gather.1
  226.1 45.9 reduce-scatter.1
where the time goes:
time: 281 us
  waiting for transfers between devices  203 us (72%)
  blocking collectives  42.2 us (15%)
  between operations  14.8 us (5%)
  other arithmetic  11 us (4%)
  matrix products  9.65 us (3%)
    all_gather x1, waiting for transfers between devices, body(): lax.all_gather(weight, 'dp', axis=0, tiled=True)  157 us
    reduce_scatter x1, waiting for transfers between devices, body(): lax.psum_scatter(partial_out, 'mp', scatter_dimension=1, tiled=True)  46.1 us
    psum x1, blocking collectives, body(): lax.psum((column_part, weighted_part), ('dp', 'mp'))  42.2 us
    dot_general x1, matrix products, body(): jnp.dot(hidden, lax.all_gather(weight, 'dp', axis=0, tiled=True), preferr...  9.65 us
  transfers between devices with their start and end apart: 2, of which 2 were waited for; matrix products, arithmetic and copies ran while one was open for 0% of the time, Pallas kernels for 0%

commit v1 on v0

v1 whole, which is shorter than its diff:
```python
import functools

import jax
import jax.numpy as jnp
from jax import lax
from jax.experimental import pallas as pl
from jax.experimental.pallas import tpu as pltpu
from jax.sharding import PartitionSpec as P

D = 4096
FFW = 5376
STEP = 10
KEEP = 1.0 - STEP ** (-0.8)
RATE = min(0.01, STEP ** (-0.5))
MESH = pl.DeviceIdType.MESH
NX = 2
NZ = 4
NC = 4


def up(n, m):
    return (n + m - 1) // m * m


def kernel(
    hid_ref, master_ref, grad_ref, rf_ref, cf_ref,
    out_ref, upd_ref, row_ref, col_ref,
    hfull, wsend, wfull, acc, wacc, statz, statp, mult, psend, precv,
    s_statz, r_statz, s_statp, r_statp, s_hz, r_hz, s_hy, r_hy, s_hc, r_hc, s_w, r_w, s_p, r_p,
):
    rows, d = grad_ref.shape
    tok = hid_ref.shape[1]
    kp = hid_ref.shape[2]
    rp = wsend.shape[2]
    cw = wsend.shape[3]
    nb = NC * cw
    ffw = rows * NX * NZ * 4
    dp = lax.axis_index("dp")
    mp = lax.axis_index("mp")
    z, x = dp // NX, dp % NX
    y, c = mp // 2, mp % 2

    def dev(z_=None, x_=None, mp_=None):
        z_ = z if z_ is None else z_
        x_ = x if x_ is None else x_
        mp_ = mp if mp_ is None else mp_
        return {"dp": z_ * NX + x_, "mp": mp_}

    def flip(dy, dc):
        return (y + dy) % 2 * 2 + (c + dc) % 2

    def copy(src, dst, ssem, rsem, to):
        return pltpu.make_async_remote_copy(
            src_ref=src, dst_ref=dst, send_sem=ssem, recv_sem=rsem, device_id=to, device_id_type=MESH
        )

    zpeers = [(z + k) % NZ for k in range(1, NZ)]
    layer = [(dx, dy, dc) for dx in range(2) for dy in range(2) for dc in range(2)][1:]
    barrier = pltpu.get_barrier_semaphore()
    for zz in zpeers:
        pl.semaphore_signal(barrier, inc=1, device_id=dev(z_=zz), device_id_type=MESH)
    for dx, dy, dc in layer:
        pl.semaphore_signal(
            barrier, inc=1, device_id=dev(x_=(x + dx) % 2, mp_=flip(dy, dc)), device_id_type=MESH
        )

    acc[...] = jnp.zeros_like(acc)
    wacc[...] = jnp.zeros_like(wacc)

    def stat_step(i, carry):
        r = pl.ds(pl.multiple_of(i * 8, 8), 8)
        g = grad_ref[r, :]
        g2 = g * g
        sq = g2 + 1e-30
        rn = KEEP * rf_ref[r, :] + (1.0 - KEEP) * (jnp.sum(sq, axis=1, keepdims=True) / float(d))
        row_ref[r, :] = rn
        acc[...] += sq
        wacc[...] += g2 * (1.0 / rn)
        return carry

    lax.fori_loop(0, rows // 8, stat_step, 0)
    pa = jnp.sum(acc[...], axis=0, keepdims=True)
    pw = jnp.sum(wacc[...], axis=0, keepdims=True)
    q = d // 4
    for j in range(4):
        statz[z, j : j + 1, :] = pa[:, j * q : (j + 1) * q]
        statz[z, 4 + j : 5 + j, :] = pw[:, j * q : (j + 1) * q]
    wsend[...] = jnp.zeros_like(wsend)
    for k in range(NC):
        for m in range(4):
            wfull[k, m * kp + 2 * rp : (m + 1) * kp, :] = jnp.zeros((kp - 2 * rp, cw), wfull.dtype)

    pl.semaphore_wait(barrier, NZ - 1 + 7)

    stz = [
        copy(statz.at[z], statz.at[z], s_statz.at[k], r_statz.at[k], dev(z_=zz))
        for k, zz in enumerate(zpeers)
    ]
    for s in stz:
        s.start()
    my_lane = pl.ds(pl.multiple_of(mp * kp, 128), kp)
    hz = [
        copy(hid_ref.at[zz], hfull.at[z, :, my_lane], s_hz.at[k], r_hz.at[k], dev(z_=zz))
        for k, zz in enumerate(zpeers)
    ]
    for h in hz:
        h.start()
    hfull[z, :, my_lane] = hid_ref[z]
    for s in stz:
        s.wait()
    total = ((statz[0] + statz[1]) + statz[2]) + statz[3]
    for k, to in enumerate((dev(mp_=flip(1, 0)), dev(x_=1 - x), dev(mp_=flip(0, 1)))):
        statp[k, 0] = total
        s = copy(statp.at[k, 0], statp.at[k, 1], s_statp.at[k], r_statp.at[k], to)
        s.start()
        s.wait()
        total = total + statp[k, 1]
    for j in range(4):
        cols = slice(j * q, (j + 1) * q)
        col_ref[:, cols] = KEEP * cf_ref[:, cols] + (1.0 - KEEP) * total[j : j + 1, :] / float(ffw)
        acc[0:1, cols] = total[4 + j : 5 + j, :]
    square_total = jnp.sum(acc[0:1, :] / col_ref[...], axis=1, keepdims=True)
    root_mean = jnp.sqrt(square_total / float(ffw * d))
    mult[...] = 1.0 / jnp.maximum(1.0, root_mean)

    my_rows = pl.ds(pl.multiple_of(mp * kp + x * rp, 16), rp)

    def w_copy(k, n):
        dx, dy, dc = layer[n]
        j = flip(dy, dc)
        return copy(
            wsend.at[k, j], wfull.at[k, my_rows, :], s_w.at[k, n], r_w.at[k, n],
            dev(x_=(x + dx) % 2, mp_=j),
        )

    def weights(k, carry):
        def block(j, carry):
            cols = pl.ds(pl.multiple_of(j * nb + k * cw, 128), cw)
            scaled = grad_ref[:, cols] * lax.rsqrt(row_ref[...] * col_ref[:, cols])
            u = scaled * mult[...]
            upd_ref[:, cols] = u
            wsend[k, j, 0:rows, :] = (master_ref[:, cols] - RATE * u).astype(jnp.bfloat16)
            return carry

        lax.fori_loop(0, 4, block, 0)
        for n in range(len(layer)):
            w_copy(k, n).start()
        wfull[k, my_rows, :] = wsend[k, mp]
        return carry

    lax.fori_loop(0, NC, weights, 0)

    other_lane = pl.ds(pl.multiple_of(flip(1, 0) * kp, 128), kp)
    order = [z] + [(z - k) % NZ for k in range(1, NZ)]
    hy, hc = [], []
    for k, t in enumerate(order):
        if k:
            hz[k - 1].wait_recv()
        part = hfull.at[t, :, my_lane]
        hy.append(copy(part, part, s_hy.at[k], r_hy.at[k], dev(mp_=flip(1, 0))))
        hc.append(copy(part, part, s_hc.at[0, k], r_hc.at[0, k], dev(mp_=flip(0, 1))))
        hy[-1].start()
        hc[-1].start()
    for k, t in enumerate(order):
        hy[k].wait_recv()
        part = hfull.at[t, :, other_lane]
        hc.append(copy(part, part, s_hc.at[1, k], r_hc.at[1, k], dev(mp_=flip(0, 1))))
        hc[-1].start()
    for h in hc:
        h.wait_recv()

    def product(k, t):
        return jnp.dot(hfull[t], wfull[k], preferred_element_type=jnp.float32)

    def p_copy(k, way, dist):
        step = 1 if way == 0 else -1
        slot = way * 3 + (dist - 1)
        land = slot
        return copy(
            psend.at[k, slot], precv.at[k, land], s_p.at[k, slot], r_p.at[k, land],
            dev(z_=jnp.clip(z + step, 0, NZ - 1)),
        )

    def p_wait(k, way, dist):
        slot = way * 3 + dist - 1
        copy(psend.at[k, slot], precv.at[k, slot], s_p.at[k, slot], r_p.at[k, slot], dev(z_=(z + 1) % NZ)).wait_recv()

    def inside(way, dist):
        return z + dist <= NZ - 1 if way == 0 else z - dist >= 0

    def has_before(way):
        return z > 0 if way == 0 else z < NZ - 1

    def send_step(k, carry):
        for n in range(len(layer)):
            w_copy(k, n).wait_recv()
        for dist in range(NZ - 1, 0, -1):
            for way in range(2):
                @pl.when(inside(way, dist))
                def _():
                    t = z + dist if way == 0 else z - dist
                    part = product(k, t)
                    slot = way * 3 + dist - 1
                    if dist < NZ - 1:
                        @pl.when(has_before(way))
                        def _():
                            p_wait(k, way, dist + 1)
                            psend[k, slot] = (part + precv[k, slot + 1].astype(jnp.float32)).astype(jnp.bfloat16)

                        @pl.when(jnp.logical_not(has_before(way)))
                        def _():
                            psend[k, slot] = part.astype(jnp.bfloat16)
                    else:
                        psend[k, slot] = part.astype(jnp.bfloat16)
                    p_copy(k, way, dist).start()
        return carry

    lax.fori_loop(0, NC, send_step, 0)

    for k in range(NC):
        cols = slice(k * cw, (k + 1) * cw)
        acc2 = product(k, z)
        for way in range(2):
            @pl.when(has_before(way))
            def _():
                p_wait(k, way, 1)

            acc2 = acc2 + jnp.where(has_before(way), precv[k, way * 3].astype(jnp.float32), 0.0)
        out_ref[:, cols] = acc2.astype(out_ref.dtype)

    def drain(k, carry):
        for n in range(len(layer)):
            w_copy(k, n).wait_send()
        for dist in range(NZ - 1, 0, -1):
            for way in range(2):
                @pl.when(inside(way, dist))
                def _():
                    p_copy(k, way, dist).wait_send()
        return carry

    lax.fori_loop(0, NC, drain, 0)
    for h in hz + hy + hc:
        h.wait_send()


def fast_body(hidden, master, grad, row_factor, col_factor):
    tok, kin = hidden.shape
    rows, d = grad.shape
    rp = up(rows, 16)
    kp = up(NX * rp, 128)
    nb = d // 4
    cw = nb // NC
    h = hidden.reshape(tok, NZ, NX, rows)
    h = jnp.pad(h, ((0, 0), (0, 0), (0, 0), (0, rp - rows))).reshape(tok, NZ, NX * rp)
    h = jnp.pad(h, ((0, 0), (0, 0), (0, kp - NX * rp))).transpose(1, 0, 2)
    dma = pltpu.SemaphoreType.DMA
    bf, f32 = jnp.bfloat16, jnp.float32
    vmem = pl.BlockSpec(memory_space=pltpu.VMEM)
    out, upd, row, col = pl.pallas_call(
        kernel,
        out_shape=(
            jax.ShapeDtypeStruct((tok, nb), bf),
            jax.ShapeDtypeStruct((rows, d), f32),
            jax.ShapeDtypeStruct((rows, 1), f32),
            jax.ShapeDtypeStruct((1, d), f32),
        ),
        in_specs=[vmem] * 5,
        out_specs=(vmem,) * 4,
        scratch_shapes=[
            pltpu.VMEM((NZ, tok, 4 * kp), bf),
            pltpu.VMEM((NC, 4, rp, cw), bf),
            pltpu.VMEM((NC, 4 * kp, cw), bf),
            pltpu.VMEM((8, d), f32),
            pltpu.VMEM((8, d), f32),
            pltpu.VMEM((NZ, 8, d // 4), f32),
            pltpu.VMEM((3, 2, 8, d // 4), f32),
            pltpu.VMEM((1, 1), f32),
            pltpu.VMEM((NC, 6, tok, cw), bf),
            pltpu.VMEM((NC, 6, tok, cw), bf),
            dma((3,)), dma((3,)), dma((3,)), dma((3,)),
            dma((3,)), dma((3,)), dma((4,)), dma((4,)), dma((2, 4)), dma((2, 4)),
            dma((NC, 7)), dma((NC, 7)), dma((NC, 6)), dma((NC, 6)),
        ],
        compiler_params=pltpu.CompilerParams(
            collective_id=0, has_side_effects=True, vmem_limit_bytes=60 * 1024 * 1024
        ),
    )(h, master, grad, row_factor[:, None], col_factor[None, :])
    return out, upd, row[:, 0], col[0]


def plain_body(hidden, master, grad, row_factor, col_factor):
    squared = grad * grad + 1e-30
    row_new = KEEP * row_factor + (1.0 - KEEP) * jnp.mean(squared, axis=1)
    column_part = jnp.sum(squared, axis=0)
    weighted_part = jnp.sum(grad * grad / row_new[:, None], axis=0)
    column_total, weighted_total = lax.psum((column_part, weighted_part), ("dp", "mp"))
    col_new = KEEP * col_factor + (1.0 - KEEP) * column_total / float(FFW)
    scaled = grad * lax.rsqrt(row_new[:, None] * col_new[None, :])
    root_mean = jnp.sqrt(jnp.sum(weighted_total / col_new) / float(FFW * D))
    update = scaled / jnp.maximum(1.0, root_mean)
    weight = (master - RATE * update).astype(jnp.bfloat16)
    partial_out = jnp.dot(
        hidden, lax.all_gather(weight, "dp", axis=0, tiled=True), preferred_element_type=jnp.float32
    )
    ffn_out = lax.psum_scatter(partial_out, "mp", scatter_dimension=1, tiled=True)
    return ffn_out.astype(jnp.bfloat16), update, row_new, col_new


def solution(mesh):
    fits = mesh.shape["dp"] == NX * NZ and mesh.shape["mp"] == 4
    return jax.shard_map(
        fast_body if fits else plain_body,
        mesh=mesh,
        in_specs=(
            P("dp", "mp"),
            P(("mp", "dp"), None),
            P(("mp", "dp"), None),
            P(("mp", "dp")),
            P(),
        ),
        out_specs=(P("dp", "mp"), P(("mp", "dp"), None), P(("mp", "dp")), P()),
        check_vma=False,
    )
```

time: 281 us -> 137 us (0.49)
  waiting for transfers between devices: 203 us -> 0 us
  Pallas kernels: 0 us -> 123 us
  blocking collectives: 42.2 us -> 0 us
  between operations: 14.8 us -> 0.67 us
  local copies, waits for them, and re-layouts: 0.34 us -> 11.4 us
  matrix products: 9.65 us -> 0 us
  other arithmetic: 11 us -> 1.57 us
    all_gather x1 -> x0, waiting for transfers between devices: 157 us -> none  [body(): lax.all_gather(weight, 'dp', axis=0, tiled=True)]
    pallas_call x0 -> x1, Pallas kernels: none -> 123 us  [fast_body(): pl.pallas_call(kernel, out_shape=(jax.ShapeDtypeStruct((tok, nb), bf), ja...]
    reduce_scatter x1 -> x0, waiting for transfers between devices: 46.1 us -> none  [body(): lax.psum_scatter(partial_out, 'mp', scatter_dimension=1, tiled=True)]
    psum x1 -> x0, blocking collectives: 42.2 us -> none  [body(): lax.psum((column_part, weighted_part), ('dp', 'mp'))]
    dot_general x1 -> x0, matrix products: 9.65 us -> none  [body(): jnp.dot(hidden, lax.all_gather(weight, 'dp', axis=0, tiled=True), preferr...]
    unnamed x12 -> x6, local copies, waits for them, and re-layouts: 0.34 us -> 8.17 us
    convert_element_type x2 -> x0, other arithmetic: 7.58 us -> none  [the longest x1 5.41 us: body(): weight = (master - step_rate * update).astype(jnp.bfloat16)]
    reduce_sum x3 -> x0, other arithmetic: 3.42 us -> none  [the longest x1 2.29 us: body(): row_new = keep * row_factor + (1.0 - keep) * jnp.mean(squared, axis=1)]
  transfers between devices with their start and end apart: 2 -> 0, of which waited for: 2 -> 0; matrix products, arithmetic and copies ran while one was open for 0% -> 0% of each run, Pallas kernels for 0% -> 0%
where the time goes in v1:
time: 137 us
  Pallas kernels  123 us (90%)
  local copies, waits for them, and re-layouts  11.4 us (8%)
  other arithmetic  1.57 us (1%)
    pallas_call x1, Pallas kernels, fast_body(): pl.pallas_call(kernel, out_shape=(jax.ShapeDtypeStruct((tok, nb), bf), ja...  123 us
    unnamed x6, local copies, waits for them, and re-layouts  8.17 us

profile of v1, /device:TPU:0, one launch (start us, length us, event | category | flops | bytes accessed | tf_op | source)
XLA Modules:
  0.0 136.9 jit_solution(15257025180751449805)
XLA Ops:
  0.6 1.4 %copy.12.rf_ref = f32[168,1]{1,0:T(8,128)} copy(f32[168,1]{0,1:T(1,128)} %bitcast.11) | data formatting | bytes 1344 | tf_op jit(solution)/shard_map/broadcast_in_dim | solution.py:287
  2.1 2.0 %copy.10 = bf16[288,1344]{0,1:T(8,128)(2,1)S(1)} copy(bf16[288,1344]{1,0:T(8,128)(2,1)} %param.5) | data formatting | bytes 1548288 | tf_op args[0]
  4.1 0.1 pad.8
  4.2 0.7 copy.11
  4.9 1.0 pad_bitcast_fusion.hid_ref
  5.9 123.2 %shard_map.84 = (bf16[288,1024]{1,0:T(8,128)(2,1)}, f32[168,4096]{1,0:T(8,128)}, f32[168,1]{1,0:T(8,128)}, f32[1,4096]{1,0:T(1,128)}) custom-call(bf16[4,288,384]{2,1,0:T(8,128)(2,1)} %pad_bitcast_fusion.hid_ref, f32[168,4096]{1,0:T(8,128)} %master_ref.1, f32[168,4096]{1,0:T(8,128)} %grad_ref.1, f32[168,1]{1,0:T(8,128)} %copy.12.rf_ref, f32[1,4096]{1,0:T(1,128)} %bitcast.9), custom_call_target="tpu_custom_call" | custom-call | tf_op jit(solution)/shard_map/pallas_call | solution.py:259
  129.2 1.6 %reduce = f32[168]{0:T(256)} reduce(f32[168,1]{1,0:T(8,128)} %get-tuple-element.10, f32[]{:T(128)} %constant.10), dimensions={1}, to_apply=%get-tuple-element.10.reduce_sub_computation | reduce | bytes 1348 | tf_op jit(solution)/shard_map/pallas_call | solution.py:259
  130.7 1.9 %copy.16 = bf16[288,1024]{1,0:T(8,128)(2,1)} copy(bf16[288,1024]{1,0:T(8,128)(2,1)} %get-tuple-element.16) | data formatting | bytes 1179648
  132.7 0.0 copy-start
  132.7 3.6 %copy.17 = f32[168,4096]{1,0:T(8,128)} copy(f32[168,4096]{1,0:T(8,128)} %get-tuple-element.17) | data formatting | bytes 5505024
  136.3 0.0 copy-done
  136.3 0.6 copy.18
Async XLA Ops:
  132.7 3.6 %copy-start = (f32[1,4096]{1,0:T(1,128)S(1)}, f32[1,4096]{1,0:T(1,128)}, u32[]{:S(2)}) copy-start(f32[1,4096]{1,0:T(1,128)} %get-tuple-element.11) | copy-start | bytes 49156

commit v2 on v1

--- a/solution.py
+++ b/solution.py
@@ -55,14 +55,35 @@
         )
 
     zpeers = [(z + k) % NZ for k in range(1, NZ)]
-    layer = [(dx, dy, dc) for dx in range(2) for dy in range(2) for dc in range(2)][1:]
+    turns = [(0, 1), (1, 0), (1, 1)]
     barrier = pltpu.get_barrier_semaphore()
     for zz in zpeers:
         pl.semaphore_signal(barrier, inc=1, device_id=dev(z_=zz), device_id_type=MESH)
-    for dx, dy, dc in layer:
-        pl.semaphore_signal(
-            barrier, inc=1, device_id=dev(x_=(x + dx) % 2, mp_=flip(dy, dc)), device_id_type=MESH
-        )
+    for turn in turns:
+        pl.semaphore_signal(barrier, inc=1, device_id=dev(mp_=flip(*turn)), device_id_type=MESH)
+    pl.semaphore_signal(barrier, inc=1, device_id=dev(x_=1 - x), device_id_type=MESH)
+
+    my_lane = pl.ds(pl.multiple_of(mp * kp, 128), kp)
+    hfull[z, :, my_lane] = hid_ref[z]
+    order = [z] + [(z - k) % NZ for k in range(1, NZ)]
+    hz = [
+        copy(hid_ref.at[zz], hfull.at[z, :, my_lane], s_hz.at[k], r_hz.at[k], dev(z_=zz))
+        for k, zz in enumerate(zpeers)
+    ]
+    hy, hc = [], []
+
+    def relay(k):
+        if k:
+            hz[k - 1].wait_recv()
+        part = hfull.at[order[k], :, my_lane]
+        hy.append(copy(part, part, s_hy.at[k], r_hy.at[k], dev(mp_=flip(1, 0))))
+        hc.append(copy(part, part, s_hc.at[0, k], r_hc.at[0, k], dev(mp_=flip(0, 1))))
+        hy[-1].start()
+        hc[-1].start()
+
+    pl.semaphore_wait(barrier, NZ - 1 + 4)
+    hz[0].start()
+    relay(0)
 
     acc[...] = jnp.zeros_like(acc)
     wacc[...] = jnp.zeros_like(wacc)
@@ -90,22 +111,14 @@
         for m in range(4):
             wfull[k, m * kp + 2 * rp : (m + 1) * kp, :] = jnp.zeros((kp - 2 * rp, cw), wfull.dtype)
 
-    pl.semaphore_wait(barrier, NZ - 1 + 7)
-
     stz = [
         copy(statz.at[z], statz.at[z], s_statz.at[k], r_statz.at[k], dev(z_=zz))
         for k, zz in enumerate(zpeers)
     ]
     for s in stz:
         s.start()
-    my_lane = pl.ds(pl.multiple_of(mp * kp, 128), kp)
-    hz = [
-        copy(hid_ref.at[zz], hfull.at[z, :, my_lane], s_hz.at[k], r_hz.at[k], dev(z_=zz))
-        for k, zz in enumerate(zpeers)
-    ]
-    for h in hz:
+    for h in hz[1:]:
         h.start()
-    hfull[z, :, my_lane] = hid_ref[z]
     for s in stz:
         s.wait()
     total = ((statz[0] + statz[1]) + statz[2]) + statz[3]
@@ -123,17 +136,21 @@
     root_mean = jnp.sqrt(square_total / float(ffw * d))
     mult[...] = 1.0 / jnp.maximum(1.0, root_mean)
 
-    my_rows = pl.ds(pl.multiple_of(mp * kp + x * rp, 16), rp)
+    def rows_of(m):
+        return pl.ds(pl.multiple_of(m * kp + x * rp, 16), rp)
 
     def w_copy(k, n):
-        dx, dy, dc = layer[n]
-        j = flip(dy, dc)
-        return copy(
-            wsend.at[k, j], wfull.at[k, my_rows, :], s_w.at[k, n], r_w.at[k, n],
-            dev(x_=(x + dx) % 2, mp_=j),
-        )
-
-    def weights(k, carry):
+        if n < 3:
+            j = flip(*turns[n])
+            src, dst, to = wsend.at[k, j], wfull.at[k, rows_of(mp), :], dev(mp_=j)
+        elif n == 3:
+            src, dst, to = wsend.at[k, mp], wfull.at[k, rows_of(mp), :], dev(x_=1 - x)
+        else:
+            part = wfull.at[k, rows_of(flip(*turns[n - 4])), :]
+            src, dst, to = part, part, dev(x_=1 - x)
+        return copy(src, dst, s_w.at[k, n], r_w.at[k, n], to)
+
+    def weights(k):
         def block(j, carry):
             cols = pl.ds(pl.multiple_of(j * nb + k * cw, 128), cw)
             scaled = grad_ref[:, cols] * lax.rsqrt(row_ref[...] * col_ref[:, cols])
@@ -143,24 +160,26 @@
             return carry
 
         lax.fori_loop(0, 4, block, 0)
-        for n in range(len(layer)):
+        for n in range(4):
             w_copy(k, n).start()
-        wfull[k, my_rows, :] = wsend[k, mp]
-        return carry
-
-    lax.fori_loop(0, NC, weights, 0)
-
+        wfull[k, rows_of(mp), :] = wsend[k, mp]
+
+    def forward(k):
+        for n in range(3):
+            w_copy(k, n).wait_recv()
+            w_copy(k, 4 + n).start()
+
+    weights(0)
+    relay(1)
+    weights(1)
+    forward(0)
+    relay(2)
+    weights(2)
+    forward(1)
+    relay(3)
+    weights(3)
+    forward(2)
     other_lane = pl.ds(pl.multiple_of(flip(1, 0) * kp, 128), kp)
-    order = [z] + [(z - k) % NZ for k in range(1, NZ)]
-    hy, hc = [], []
-    for k, t in enumerate(order):
-        if k:
-            hz[k - 1].wait_recv()
-        part = hfull.at[t, :, my_lane]
-        hy.append(copy(part, part, s_hy.at[k], r_hy.at[k], dev(mp_=flip(1, 0))))
-        hc.append(copy(part, part, s_hc.at[0, k], r_hc.at[0, k], dev(mp_=flip(0, 1))))
-        hy[-1].start()
-        hc[-1].start()
     for k, t in enumerate(order):
         hy[k].wait_recv()
         part = hfull.at[t, :, other_lane]
@@ -192,7 +211,7 @@
         return z > 0 if way == 0 else z < NZ - 1
 
     def send_step(k, carry):
-        for n in range(len(layer)):
+        for n in range(3, 7):
             w_copy(k, n).wait_recv()
         for dist in range(NZ - 1, 0, -1):
             for way in range(2):
@@ -213,6 +232,11 @@
                     else:
                         psend[k, slot] = part.astype(jnp.bfloat16)
                     p_copy(k, way, dist).start()
+
+        @pl.when(k == 0)
+        def _():
+            forward(NC - 1)
+
         return carry
 
     lax.fori_loop(0, NC, send_step, 0)
@@ -229,7 +253,7 @@
         out_ref[:, cols] = acc2.astype(out_ref.dtype)
 
     def drain(k, carry):
-        for n in range(len(layer)):
+        for n in range(7):
             w_copy(k, n).wait_send()
         for dist in range(NZ - 1, 0, -1):
             for way in range(2):

time: 137 us -> 126 us (0.920)
  Pallas kernels: 123 us -> 112 us
    pallas_call x1, Pallas kernels: 123 us -> 112 us  [fast_body(): pl.pallas_call(kernel, out_shape=(jax.ShapeDtypeStruct((tok, nb), bf), ja...]
where the time goes in v2:
time: 126 us
  Pallas kernels  112 us (89%)
  local copies, waits for them, and re-layouts  11.4 us (9%)
  other arithmetic  1.57 us (1%)
    pallas_call x1, Pallas kernels, fast_body(): pl.pallas_call(kernel, out_shape=(jax.ShapeDtypeStruct((tok, nb), bf), ja...  112 us
    unnamed x6, local copies, waits for them, and re-layouts  8.17 us

profile of v2, /device:TPU:0, one launch (start us, length us, event | category | flops | bytes accessed | tf_op | source)
XLA Modules:
  0.0 125.8 jit_solution(7646749626181827432)
XLA Ops:
  0.6 1.4 %copy.12.rf_ref = f32[168,1]{1,0:T(8,128)} copy(f32[168,1]{0,1:T(1,128)} %bitcast.11) | data formatting | bytes 1344 | tf_op jit(solution)/shard_map/broadcast_in_dim | solution.py:311
  2.1 2.0 %copy.10 = bf16[288,1344]{0,1:T(8,128)(2,1)S(1)} copy(bf16[288,1344]{1,0:T(8,128)(2,1)} %param.5) | data formatting | bytes 1548288 | tf_op args[0]
  4.1 0.1 pad.8
  4.2 0.7 copy.11
  4.9 1.0 pad_bitcast_fusion.hid_ref
  5.9 112.2 %shard_map.84 = (bf16[288,1024]{1,0:T(8,128)(2,1)}, f32[168,4096]{1,0:T(8,128)}, f32[168,1]{1,0:T(8,128)}, f32[1,4096]{1,0:T(1,128)}) custom-call(bf16[4,288,384]{2,1,0:T(8,128)(2,1)} %pad_bitcast_fusion.hid_ref, f32[168,4096]{1,0:T(8,128)} %master_ref.1, f32[168,4096]{1,0:T(8,128)} %grad_ref.1, f32[168,1]{1,0:T(8,128)} %copy.12.rf_ref, f32[1,4096]{1,0:T(1,128)} %bitcast.9), custom_call_target="tpu_custom_call" | custom-call | tf_op jit(solution)/shard_map/pallas_call | solution.py:283
  118.1 1.6 %reduce = f32[168]{0:T(256)} reduce(f32[168,1]{1,0:T(8,128)} %get-tuple-element.10, f32[]{:T(128)} %constant.10), dimensions={1}, to_apply=%get-tuple-element.10.reduce_sub_computation | reduce | bytes 1348 | tf_op jit(solution)/shard_map/pallas_call | solution.py:283
  119.7 1.9 %copy.16 = bf16[288,1024]{1,0:T(8,128)(2,1)} copy(bf16[288,1024]{1,0:T(8,128)(2,1)} %get-tuple-element.16) | data formatting | bytes 1179648
  121.6 0.0 copy-start
  121.6 3.6 %copy.17 = f32[168,4096]{1,0:T(8,128)} copy(f32[168,4096]{1,0:T(8,128)} %get-tuple-element.17) | data formatting | bytes 5505024
  125.2 0.0 copy-done
  125.2 0.6 copy.18
Async XLA Ops:
  121.6 3.6 %copy-start = (f32[1,4096]{1,0:T(1,128)S(1)}, f32[1,4096]{1,0:T(1,128)}, u32[]{:S(2)}) copy-start(f32[1,4096]{1,0:T(1,128)} %get-tuple-element.11) | copy-start | bytes 49156

commit v3 on v2

--- a/solution.py
+++ b/solution.py
@@ -25,7 +25,7 @@
 def kernel(
     hid_ref, master_ref, grad_ref, rf_ref, cf_ref,
     out_ref, upd_ref, row_ref, col_ref,
-    hfull, wsend, wfull, acc, wacc, statz, statp, mult, psend, precv,
+    hfull, wsend, wfull, acc, wacc, statz, statp, mult, psend, precv, own,
     s_statz, r_statz, s_statp, r_statp, s_hz, r_hz, s_hy, r_hy, s_hc, r_hc, s_w, r_w, s_p, r_p,
 ):
     rows, d = grad_ref.shape
@@ -237,13 +237,14 @@
         def _():
             forward(NC - 1)
 
+        own[k] = product(k, z)
         return carry
 
     lax.fori_loop(0, NC, send_step, 0)
 
     for k in range(NC):
         cols = slice(k * cw, (k + 1) * cw)
-        acc2 = product(k, z)
+        acc2 = own[k]
         for way in range(2):
             @pl.when(has_before(way))
             def _():
@@ -301,6 +302,7 @@
             pltpu.VMEM((1, 1), f32),
             pltpu.VMEM((NC, 6, tok, cw), bf),
             pltpu.VMEM((NC, 6, tok, cw), bf),
+            pltpu.VMEM((NC, tok, cw), f32),
             dma((3,)), dma((3,)), dma((3,)), dma((3,)),
             dma((3,)), dma((3,)), dma((4,)), dma((4,)), dma((2, 4)), dma((2, 4)),
             dma((NC, 7)), dma((NC, 7)), dma((NC, 6)), dma((NC, 6)),

time: 126 us -> 126 us (level)
  no operation moved by 1% of the time
where the time goes in v3:
time: 126 us
  Pallas kernels  112 us (89%)
  local copies, waits for them, and re-layouts  11.4 us (9%)
  other arithmetic  1.57 us (1%)
    pallas_call x1, Pallas kernels, fast_body(): pl.pallas_call(kernel, out_shape=(jax.ShapeDtypeStruct((tok, nb), bf), ja...  112 us
    unnamed x6, local copies, waits for them, and re-layouts  8.17 us

profile of v3, /device:TPU:0, one launch (start us, length us, event | category | flops | bytes accessed | tf_op | source)
XLA Modules:
  0.0 125.8 jit_solution(8067538595427272632)
XLA Ops:
  0.6 1.4 %copy.12.rf_ref = f32[168,1]{1,0:T(8,128)} copy(f32[168,1]{0,1:T(1,128)} %bitcast.11) | data formatting | bytes 1344 | tf_op jit(solution)/shard_map/broadcast_in_dim | solution.py:313
  2.1 2.0 %copy.10 = bf16[288,1344]{0,1:T(8,128)(2,1)S(1)} copy(bf16[288,1344]{1,0:T(8,128)(2,1)} %param.5) | data formatting | bytes 1548288 | tf_op args[0]
  4.1 0.1 pad.8
  4.2 0.7 copy.11
  4.9 1.0 pad_bitcast_fusion.hid_ref
  5.9 112.2 %shard_map.84 = (bf16[288,1024]{1,0:T(8,128)(2,1)}, f32[168,4096]{1,0:T(8,128)}, f32[168,1]{1,0:T(8,128)}, f32[1,4096]{1,0:T(1,128)}) custom-call(bf16[4,288,384]{2,1,0:T(8,128)(2,1)} %pad_bitcast_fusion.hid_ref, f32[168,4096]{1,0:T(8,128)} %master_ref.1, f32[168,4096]{1,0:T(8,128)} %grad_ref.1, f32[168,1]{1,0:T(8,128)} %copy.12.rf_ref, f32[1,4096]{1,0:T(1,128)} %bitcast.9), custom_call_target="tpu_custom_call" | custom-call | tf_op jit(solution)/shard_map/pallas_call | solution.py:284
  118.1 1.6 %reduce = f32[168]{0:T(256)} reduce(f32[168,1]{1,0:T(8,128)} %get-tuple-element.10, f32[]{:T(128)} %constant.10), dimensions={1}, to_apply=%get-tuple-element.10.reduce_sub_computation | reduce | bytes 1348 | tf_op jit(solution)/shard_map/pallas_call | solution.py:284
  119.7 1.9 %copy.16 = bf16[288,1024]{1,0:T(8,128)(2,1)} copy(bf16[288,1024]{1,0:T(8,128)(2,1)} %get-tuple-element.16) | data formatting | bytes 1179648
  121.6 0.0 copy-start
  121.6 3.6 %copy.17 = f32[168,4096]{1,0:T(8,128)} copy(f32[168,4096]{1,0:T(8,128)} %get-tuple-element.17) | data formatting | bytes 5505024
  125.2 0.0 copy-done
  125.2 0.6 copy.18
Async XLA Ops:
  121.6 3.6 %copy-start = (f32[1,4096]{1,0:T(1,128)S(1)}, f32[1,4096]{1,0:T(1,128)}, u32[]{:S(2)}) copy-start(f32[1,4096]{1,0:T(1,128)} %get-tuple-element.11) | copy-start | bytes 49156
